TPU v7x, 32 devices: a whole 2x2x4 slice. The times are simulated.
32 devices in a mesh: tp: 8 (over y, x, core), dp: 4 (over z).
Axes of the slice: x: 2, y: 2, z: 4, core: 2. Of those that a mesh axis runs over, the one named last changes fastest.
Arguments:
- grad_out: bfloat16 [512, 16384], P('dp', 'tp'), may hold values from -6 to 6
- hidden_sum: bfloat16 [512, 16384], P('dp', 'tp'), may hold values from -100 to 100
- norm_gain: float32 [16384], P('tp'), may hold values from 0.5 to 1.5
- out_weight: bfloat16 [2048, 16384], P(None, 'tp'), may hold values from -0.046875 to 0.046875
Outputs:
- resid_grad: bfloat16 [512, 16384], P('dp', 'tp')
- attn_grad: bfloat16 [512, 2048], P('dp', 'tp')
- gain_grad: float32 [16384], P('tp')
All inputs are finite; a program needn't handle non-finite values.
Results may differ from a plain program's by a relative error of at most 0.0049.
Values sent between devices are 32-bit elements; how exact they have to be, the bound alone decides.
A program may use at most 64 MiB of HBM per device.

v0:
```python
import functools

import jax
import jax.numpy as jnp
from jax import lax
from jax.experimental import pallas as pl
from jax.experimental.pallas import tpu as pltpu
from jax.sharding import PartitionSpec as P

EPSILON = 1e-05
MESH = pl.DeviceIdType.MESH
LANES = 128
CHUNKS = 1


def flipped(index, mask):
    result, bit = index, 1
    while bit <= mask:
        if mask & bit:
            result = result + bit * (1 - 2 * lax.rem(lax.div(index, bit), 2))
        bit *= 2
    return result


def kernel(
    tp, dp, features,
    grad_hbm, hidden_hbm, gain_hbm, weight_hbm,
    resid, attn, gain_out,
    grad, both, gain_ref, weight, stats, pair_out, pair_in, pair_own, chip_out, chip_in, relay_in, sums,
    load_sem, weight_sem,
    stat_send, stat_recv, pair_send, pair_recv, chip_send, chip_recv,
    relay_send, relay_recv, sum_send, sum_recv,
):
    me = lax.axis_index("tp")
    z = lax.axis_index("dp")
    rows, width = grad.shape
    block = attn.shape[1]
    hidden = both.at[pl.ds(rows, rows), :]
    steps = width // LANES

    load_grad = pltpu.make_async_copy(grad_hbm, grad, load_sem.at[0])
    load_hidden = pltpu.make_async_copy(hidden_hbm, hidden, load_sem.at[1])
    load_gain = pltpu.make_async_copy(gain_hbm, gain_ref, load_sem.at[2])
    load_hidden.start()
    load_grad.start()
    load_gain.start()

    barrier = pltpu.get_barrier_semaphore()
    for mask in range(1, tp):
        pl.semaphore_signal(
            barrier, inc=1, device_id={"tp": flipped(me, mask)}, device_id_type=MESH
        )
    for step in range(1, dp):
        pl.semaphore_signal(
            barrier, inc=1, device_id={"dp": lax.rem(z + step, dp)}, device_id_type=MESH
        )

    order = sorted(range(0, tp, 2), key=lambda mask: (-bin(mask).count("1"), mask))

    def weight_rows(mask):
        return pl.ds(pl.multiple_of(flipped(me, mask) * block, block), block)

    weight_loads = {}
    for chip in order:
        for mask in (chip ^ 1, chip):
            at = weight_rows(mask)
            weight_loads[mask] = pltpu.make_async_copy(
                weight_hbm.at[at, :], weight.at[mask], weight_sem.at[mask]
            )
            weight_loads[mask].start()

    load_gain.wait()
    load_hidden.wait()
    load_grad.wait()
    squares = jnp.zeros((rows, LANES), jnp.float32)
    dotted = jnp.zeros((rows, LANES), jnp.float32)
    for k in range(steps):
        at = slice(k * LANES, (k + 1) * LANES)
        h = hidden[:, at].astype(jnp.float32)
        g = grad[:, at].astype(jnp.float32)
        squares += h * h
        dotted += gain_ref[:, at] * g * h
    local_factor = jnp.sum(dotted, axis=1, keepdims=True) / (
        jnp.sum(squares, axis=1, keepdims=True) + width * EPSILON
    )
    stats[0, 0:1, :] = jnp.sum(squares.T, axis=0, keepdims=True)
    stats[0, 1:2, :] = jnp.sum(dotted.T, axis=0, keepdims=True)

    pl.semaphore_wait(barrier, tp - 1 + dp - 1)
    stat_copies = []
    for mask in sorted(range(1, tp), key=lambda mask: (-bin(mask).count("1"), mask)):
        copy = pltpu.make_async_remote_copy(
            src_ref=stats.at[0],
            dst_ref=stats.at[mask],
            send_sem=stat_send.at[mask],
            recv_sem=stat_recv.at[mask],
            device_id={"tp": flipped(me, mask)},
            device_id_type=MESH,
        )
        copy.start()
        stat_copies.append(copy)
    for k in range(steps):
        at = slice(k * LANES, (k + 1) * LANES)
        h = hidden[:, at].astype(jnp.float32)
        g = grad[:, at].astype(jnp.float32)
        both[0:rows, at] = (gain_ref[:, at] * g - h * local_factor).astype(jnp.bfloat16)

    def products(mask, target):
        out = lax.dot_general(
            both[...],
            weight[mask],
            (((1,), (1,)), ((), ())),
            preferred_element_type=jnp.float32,
        )
        target[0] = out[0:rows] + local_factor * out[rows:]
        target[1] = out[rows:]

    pair_copies = []

    def pair_step(slot):
        chip = order[slot]
        weight_loads[chip ^ 1].wait()
        weight_loads[chip].wait()
        products(chip ^ 1, pair_out.at[slot])
        copy = pltpu.make_async_remote_copy(
            src_ref=pair_out.at[slot],
            dst_ref=pair_in.at[slot],
            send_sem=pair_send.at[slot],
            recv_sem=pair_recv.at[slot],
            device_id={"tp": flipped(me, 1)},
            device_id_type=MESH,
        )
        products(chip, pair_own.at[slot])
        copy.start()
        pair_copies.append(copy)

    last = len(order) - 1
    for slot in range(last):
        pair_step(slot)

    for copy in stat_copies:
        copy.wait_recv()
    total = stats[0]
    for mask in range(1, tp):
        total = total + stats[mask]
    inverse_row = lax.rsqrt(total[0:1, :] / features + EPSILON)
    factor_row = inverse_row * inverse_row * total[1:2, :] / features
    inverse = jnp.broadcast_to(inverse_row, (LANES, rows)).T
    factor = jnp.broadcast_to(factor_row, (LANES, rows)).T

    pieces = block // LANES
    relayed = len(order) == 4 and pieces % 2 == 0
    chunk = rows // CHUNKS

    def chip_piece(slot, piece):
        at = slice(piece * LANES, (piece + 1) * LANES)
        gained = pair_own[slot, 0, :, at] + pair_in[slot, 0, :, at]
        plain = pair_own[slot, 1, :, at] + pair_in[slot, 1, :, at]
        chip_out[slot, piece] = inverse * (gained - factor * plain)

    def send(slot, piece, part):
        at = pl.ds(part * chunk, chunk)
        copy = pltpu.make_async_remote_copy(
            src_ref=chip_out.at[slot, piece, at],
            dst_ref=chip_in.at[slot, piece, at],
            send_sem=chip_send.at[slot, piece, part],
            recv_sem=chip_recv.at[slot, piece, part],
            device_id={"tp": flipped(me, order[slot])},
            device_id_type=MESH,
        )
        copy.start()
        return copy

    def pass_on(piece, part):
        at = pl.ds(part * chunk, chunk)
        copy = pltpu.make_async_remote_copy(
            src_ref=chip_out.at[0, piece, at],
            dst_ref=relay_in.at[piece, at],
            send_sem=relay_send.at[piece, part],
            recv_sem=relay_recv.at[piece, part],
            device_id={"tp": flipped(me, order[1 + piece % 2])},
            device_id_type=MESH,
        )
        copy.start()
        return copy

    chip_copies, relay_copies = [], []
    pair_copies[0].wait_recv()
    for piece in range(pieces):
        chip_piece(0, piece)
        for part in range(CHUNKS):
            if relayed:
                relay_copies.append((piece, part, pass_on(piece, part)))
            else:
                chip_copies.append(send(0, piece, part))
    for slot in range(1, last):
        pair_copies[slot].wait_recv()
        for piece in range(pieces):
            chip_piece(slot, piece)
            if not relayed or piece % 2 == slot - 1:
                for part in range(CHUNKS):
                    chip_copies.append(send(slot, piece, part))

    for k in range(steps):
        at = slice(k * LANES, (k + 1) * LANES)
        h = hidden[:, at].astype(jnp.float32)
        g = grad[:, at].astype(jnp.float32)
        sums[0, :, at] = jnp.sum(g * h * inverse, axis=0, keepdims=True)
    sum_copies = []
    for step in range(dp - 1, 0, -1):
        copy = pltpu.make_async_remote_copy(
            src_ref=sums.at[0],
            dst_ref=sums.at[step],
            send_sem=sum_send.at[step],
            recv_sem=sum_recv.at[step],
            device_id={"dp": lax.rem(z + step, dp)},
            device_id_type=MESH,
        )
        copy.start()
        sum_copies.append(copy)

    pair_step(last)

    for k in range(steps):
        at = slice(k * LANES, (k + 1) * LANES)
        h = hidden[:, at].astype(jnp.float32)
        g = grad[:, at].astype(jnp.float32)
        value = inverse * (gain_ref[:, at] * g - h * factor)
        resid[:, at] = value.astype(jnp.bfloat16)

    for part in range(CHUNKS):
        for piece, own_part, copy in relay_copies:
            if own_part == part:
                slot = 2 - piece % 2
                at = slice(part * chunk, (part + 1) * chunk)
                copy.wait_recv()
                chip_out[slot, piece, at] = chip_out[slot, piece, at] + relay_in[piece, at]
                chip_copies.append(send(slot, piece, part))

    pair_copies[last].wait_recv()
    for piece in range(pieces):
        chip_piece(last, piece)

    for copy in sum_copies:
        copy.wait_recv()
    gain_total = sums[0]
    for step in range(1, dp):
        gain_total = gain_total + sums[step]
    gain_out[...] = gain_total

    for copy in chip_copies:
        copy.wait_recv()
    for piece in range(pieces):
        result = chip_out[last, piece]
        for slot in range(1 if relayed else 0, last):
            result = result + chip_in[slot, piece]
        attn[:, piece * LANES : (piece + 1) * LANES] = result

    for copy in stat_copies + pair_copies + chip_copies + sum_copies:
        copy.wait_send()
    for _, _, copy in relay_copies:
        copy.wait_send()


def write_results(resid, attn, gain, resid_out, attn_out, gain_out):
    resid_out[...] = resid[...]
    attn_out[...] = attn[...].astype(jnp.bfloat16)
    gain_out[...] = gain[...]


def on_device(tp, dp, features, grad_out, hidden_sum, norm_gain, out_weight):
    rows, width = grad_out.shape
    block = out_weight.shape[0] // tp
    half = tp // 2
    pieces = block // LANES
    anywhere = pl.BlockSpec(memory_space=pltpu.HBM)
    vmem = pl.BlockSpec(memory_space=pltpu.VMEM)
    dma = pltpu.SemaphoreType.DMA
    resid, attn, gain = pl.pallas_call(
        functools.partial(kernel, tp, dp, features),
        out_shape=(
            jax.ShapeDtypeStruct((rows, width), jnp.bfloat16),
            jax.ShapeDtypeStruct((rows, block), jnp.float32),
            jax.ShapeDtypeStruct((1, width), jnp.float32),
        ),
        in_specs=[anywhere, anywhere, anywhere, anywhere],
        out_specs=(vmem, vmem, vmem),
        scratch_shapes=[
            pltpu.VMEM((rows, width), jnp.bfloat16),
            pltpu.VMEM((2 * rows, width), jnp.bfloat16),
            pltpu.VMEM((1, width), jnp.float32),
            pltpu.VMEM((tp, block, width), jnp.bfloat16),
            pltpu.VMEM((tp, 2, rows), jnp.float32),
            pltpu.VMEM((half, 2, rows, block), jnp.float32),
            pltpu.VMEM((half, 2, rows, block), jnp.float32),
            pltpu.VMEM((half, 2, rows, block), jnp.float32),
            pltpu.VMEM((half, pieces, rows, LANES), jnp.float32),
            pltpu.VMEM((half, pieces, rows, LANES), jnp.float32),
            pltpu.VMEM((pieces, rows, LANES), jnp.float32),
            pltpu.VMEM((dp, 1, width), jnp.float32),
            dma((3,)),
            dma((tp,)),
            dma((tp,)),
            dma((tp,)),
            dma((half,)),
            dma((half,)),
            dma((half, pieces, CHUNKS)),
            dma((half, pieces, CHUNKS)),
            dma((pieces, CHUNKS)),
            dma((pieces, CHUNKS)),
            dma((dp,)),
            dma((dp,)),
        ],
        compiler_params=pltpu.CompilerParams(
            collective_id=0, has_side_effects=True, vmem_limit_bytes=52 * 2**20
        ),
        name="backward",
    )(
        pltpu.with_memory_space_constraint(grad_out, pltpu.HBM),
        pltpu.with_memory_space_constraint(hidden_sum, pltpu.HBM),
        pltpu.with_memory_space_constraint(norm_gain.reshape(1, width), pltpu.HBM),
        pltpu.with_memory_space_constraint(out_weight, pltpu.HBM),
    )
    resid, attn, gain = pl.pallas_call(
        write_results,
        out_shape=(
            jax.ShapeDtypeStruct((rows, width), jnp.bfloat16),
            jax.ShapeDtypeStruct((rows, block), jnp.bfloat16),
            jax.ShapeDtypeStruct((1, width), jnp.float32),
        ),
        in_specs=[vmem, vmem, vmem],
        out_specs=(vmem, vmem, vmem),
        compiler_params=pltpu.CompilerParams(vmem_limit_bytes=4 * 2**20),
        name="write_results",
    )(resid, attn, gain)
    return resid, attn, gain.reshape(width)


def solution(mesh):
    tp, dp = mesh.shape["tp"], mesh.shape["dp"]

    def whole(grad_out, hidden_sum, norm_gain, out_weight):
        features = grad_out.shape[1]
        return jax.shard_map(
            functools.partial(on_device, tp, dp, features),
            mesh=mesh,
            in_specs=(P("dp", "tp"), P("dp", "tp"), P("tp"), P(None, "tp")),
            out_specs=(P("dp", "tp"), P("dp", "tp"), P("tp")),
            check_vma=False,
        )(grad_out, hidden_sum, norm_gain, out_weight)

    return whole
```

profile of v0, /device:TPU:0, one launch (start us, length us, event | category | flops | bytes accessed | tf_op | source)
XLA Modules:
  0.0 18.5 jit_solution(15235224117046106647)
XLA Ops:
  0.6 17.0 %backward.1 = (bf16[128,2048]{1,0:T(8,128)(2,1)S(1)}, f32[128,256]{1,0:T(8,128)S(1)}, f32[1,2048]{1,0:T(1,128)S(1)}) custom-call(bf16[128,2048]{1,0:T(8,128)(2,1)} %grad_hbm.1, bf16[128,2048]{1,0:T(8,128)(2,1)} %hidden_hbm.1, f32[1,2048]{1,0:T(1,128)} %bitcast.2, bf16[2048,2048]{1,0:T(8,128)(2,1)} %weight_hbm.1), custom_call_target="tpu_custom_call" | custom-call | tf_op jit(solution)/shard_map/backward/pallas_call | solution.py:279
  17.6 0.9 %write_results.1 = (bf16[128,2048]{1,0:T(8,128)(2,1)}, bf16[128,256]{1,0:T(8,128)(2,1)}, f32[1,2048]{1,0:T(1,128)}) custom-call(bf16[128,2048]{1,0:T(8,128)(2,1)S(1)} %get-tuple-element.9.resid, f32[128,256]{1,0:T(8,128)S(1)} %get-tuple-element.10.attn, f32[1,2048]{1,0:T(1,128)S(1)} %get-tuple-element.11.gain), custom_call_target="tpu_custom_call" | custom-call | tf_op jit(solution)/shard_map/write_results/pallas_call | solution.py:324
where the time goes:
time: 18.6 us; the launch traced here: 18.5 us
  Pallas kernels  17.9 us (96%)
  between operations  0.64 us (3%)
    pallas_call x1, Pallas kernels, on_device(): pl.pallas_call(functools.partial(kernel, tp, dp, features), out_shape=(ja...  17 us
    pallas_call x1, Pallas kernels, on_device(): pl.pallas_call(write_results, out_shape=(jax.ShapeDtypeStruct((rows, widt...  0.86 us

commit v1 on v0

--- a/solution.py
+++ b/solution.py
@@ -29,7 +29,7 @@
     grad, both, gain_ref, weight, stats, pair_out, pair_in, pair_own, chip_out, chip_in, relay_in, sums,
     load_sem, weight_sem,
     stat_send, stat_recv, pair_send, pair_recv, chip_send, chip_recv,
-    relay_send, relay_recv, sum_send, sum_recv,
+    relay_send, relay_recv, sum_send, sum_recv, ready,
 ):
     me = lax.axis_index("tp")
     z = lax.axis_index("dp")
@@ -51,9 +51,13 @@
             barrier, inc=1, device_id={"tp": flipped(me, mask)}, device_id_type=MESH
         )
     for step in range(1, dp):
-        pl.semaphore_signal(
-            barrier, inc=1, device_id={"dp": lax.rem(z + step, dp)}, device_id_type=MESH
-        )
+
+        @pl.when(z + step < dp)
+        def _():
+            pl.semaphore_signal(
+                barrier, inc=1, device_id={"dp": z + step}, device_id_type=MESH
+            )
+
 
     order = sorted(range(0, tp, 2), key=lambda mask: (-bin(mask).count("1"), mask))
 
@@ -86,7 +90,7 @@
     stats[0, 0:1, :] = jnp.sum(squares.T, axis=0, keepdims=True)
     stats[0, 1:2, :] = jnp.sum(dotted.T, axis=0, keepdims=True)
 
-    pl.semaphore_wait(barrier, tp - 1 + dp - 1)
+    pl.semaphore_wait(barrier, tp - 1 + z)
     stat_copies = []
     for mask in sorted(range(1, tp), key=lambda mask: (-bin(mask).count("1"), mask)):
         copy = pltpu.make_async_remote_copy(
@@ -99,6 +103,14 @@
         )
         copy.start()
         stat_copies.append(copy)
+    for step in range(1, dp):
+
+        @pl.when(z >= step)
+        def _():
+            pl.semaphore_signal(
+                ready, inc=1, device_id={"dp": z - step}, device_id_type=MESH
+            )
+
     for k in range(steps):
         at = slice(k * LANES, (k + 1) * LANES)
         h = hidden[:, at].astype(jnp.float32)
@@ -216,7 +228,7 @@
             device_id={"dp": lax.rem(z + step, dp)},
             device_id_type=MESH,
         )
-        copy.start()
+        pl.when(z + step >= dp)(copy.start)
         sum_copies.append(copy)
 
     pair_step(last)
@@ -227,6 +239,13 @@
         g = grad[:, at].astype(jnp.float32)
         value = inverse * (gain_ref[:, at] * g - h * factor)
         resid[:, at] = value.astype(jnp.bfloat16)
+
+    @pl.when(z < dp - 1)
+    def _():
+        pl.semaphore_wait(ready, dp - 1 - z)
+
+    for step, copy in zip(range(dp - 1, 0, -1), sum_copies):
+        pl.when(z + step < dp)(copy.start)
 
     for part in range(CHUNKS):
         for piece, own_part, copy in relay_copies:
@@ -310,6 +329,7 @@
             dma((pieces, CHUNKS)),
             dma((dp,)),
             dma((dp,)),
+            pltpu.SemaphoreType.REGULAR,
         ],
         compiler_params=pltpu.CompilerParams(
             collective_id=0, has_side_effects=True, vmem_limit_bytes=52 * 2**20

time: 18.6 us -> 16.5 us (0.89)
  Pallas kernels: 17.9 us -> 15.8 us
    pallas_call x1, Pallas kernels: 17 us -> 14.9 us  [on_device(): pl.pallas_call(functools.partial(kernel, tp, dp, features), out_shape=(ja...]
where the time goes in v1:
time: 16.5 us; the launch traced here: 16.4 us
  Pallas kernels  15.8 us (96%)
  between operations  0.64 us (4%)
    pallas_call x1, Pallas kernels, on_device(): pl.pallas_call(functools.partial(kernel, tp, dp, features), out_shape=(ja...  14.9 us
    pallas_call x1, Pallas kernels, on_device(): pl.pallas_call(write_results, out_shape=(jax.ShapeDtypeStruct((rows, widt...  0.86 us

profile of v1, /device:TPU:0, one launch (start us, length us, event | category | flops | bytes accessed | tf_op | source)
XLA Modules:
  0.0 16.4 jit_solution(5987424578672657129)
XLA Ops:
  0.6 14.9 %backward.1 = (bf16[128,2048]{1,0:T(8,128)(2,1)S(1)}, f32[128,256]{1,0:T(8,128)S(1)}, f32[1,2048]{1,0:T(1,128)S(1)}) custom-call(bf16[128,2048]{1,0:T(8,128)(2,1)} %grad_hbm.1, bf16[128,2048]{1,0:T(8,128)(2,1)} %hidden_hbm.1, f32[1,2048]{1,0:T(1,128)} %bitcast.2, bf16[2048,2048]{1,0:T(8,128)(2,1)} %weight_hbm.1), custom_call_target="tpu_custom_call" | custom-call | tf_op jit(solution)/shard_map/backward/pallas_call | solution.py:298
  15.5 0.9 %write_results.1 = (bf16[128,2048]{1,0:T(8,128)(2,1)}, bf16[128,256]{1,0:T(8,128)(2,1)}, f32[1,2048]{1,0:T(1,128)}) custom-call(bf16[128,2048]{1,0:T(8,128)(2,1)S(1)} %get-tuple-element.9.resid, f32[128,256]{1,0:T(8,128)S(1)} %get-tuple-element.10.attn, f32[1,2048]{1,0:T(1,128)S(1)} %get-tuple-element.11.gain), custom_call_target="tpu_custom_call" | custom-call | tf_op jit(solution)/shard_map/write_results/pallas_call | solution.py:344

commit v2 on v1

v2 whole, which is shorter than its diff:
```python
import functools

import jax
import jax.numpy as jnp
from jax import lax
from jax.experimental import pallas as pl
from jax.experimental.pallas import tpu as pltpu
from jax.sharding import PartitionSpec as P

EPSILON = 1e-05
MESH = pl.DeviceIdType.MESH
LANES = 128
BANDS = 4


def flipped(index, mask):
    result, bit = index, 1
    while bit <= mask:
        if mask & bit:
            result = result + bit * (1 - 2 * lax.rem(lax.div(index, bit), 2))
        bit *= 2
    return result


def cuts(rows, relayed):
    if not relayed:
        return [(0, rows)]
    half, quarter = rows // 2, rows // 4
    return [(0, half), (half, quarter), (half + quarter, quarter)]


def kernel(
    tp, dp, features,
    grad_hbm, hidden_hbm, gain_hbm, weight_hbm,
    resid, attn, gain_out,
    grad, both, gain_ref, weight, stats, pair_out, pair_in, pair_own, chip_out, chip_in,
    early_out, early_in, relay_in, sums,
    load_sem, weight_sem, send_sem, stat_recv, pair_recv, early_recv, relay_recv, chip_recv,
    sum_recv, ready,
):
    me = lax.axis_index("tp")
    z = lax.axis_index("dp")
    core = lax.rem(me, 2)
    rows, width = grad.shape
    block = attn.shape[1]
    hidden = both.at[pl.ds(rows, rows), :]
    steps = width // LANES
    band = rows // BANDS
    pieces = block // LANES
    order = sorted(range(0, tp, 2), key=lambda mask: (-bin(mask).count("1"), mask))
    last = len(order) - 1
    relayed = len(order) == 4 and pieces % 2 == 0
    parts = cuts(rows, relayed)
    early = parts[0][1]

    def remote(source, target, kind, recv_sem, axis, index):
        return pltpu.make_async_remote_copy(
            src_ref=source,
            dst_ref=target,
            send_sem=send_sem.at[kind],
            recv_sem=recv_sem,
            device_id={axis: index},
            device_id_type=MESH,
        )

    def wait_bytes(ref, sem):
        pltpu.make_async_copy(ref, ref, sem).wait()

    load_gain = pltpu.make_async_copy(gain_hbm, gain_ref, load_sem.at[BANDS])
    for part in range(BANDS):
        at = pl.ds(part * band, band)
        pltpu.make_async_copy(
            hidden_hbm.at[at, :],
            both.at[pl.ds(rows + part * band, band), :],
            load_sem.at[part],
        ).start()
        pltpu.make_async_copy(grad_hbm.at[at, :], grad.at[at, :], load_sem.at[part]).start()
        if part == 0:
            load_gain.start()

    barrier = pltpu.get_barrier_semaphore()
    for mask in range(1, tp):
        pl.semaphore_signal(
            barrier, inc=1, device_id={"tp": flipped(me, mask)}, device_id_type=MESH
        )
    for step in range(1, dp):

        @pl.when(z + step < dp)
        def _():
            pl.semaphore_signal(
                barrier, inc=1, device_id={"dp": z + step}, device_id_type=MESH
            )

    weight_loads = []
    for slot, chip in enumerate(order):
        start = pl.multiple_of((flipped(me, chip) - core) * block, 2 * block)
        load = pltpu.make_async_copy(
            weight_hbm.at[pl.ds(start, 2 * block), :], weight.at[slot], weight_sem.at[slot]
        )
        load.start()
        weight_loads.append(load)

    load_gain.wait()
    squares, dotted = [], []
    for part in range(BANDS):
        wait_bytes(grad.at[pl.ds(0, 2 * band), :], load_sem.at[part])
        at_rows = slice(part * band, (part + 1) * band)
        band_squares = jnp.zeros((band, LANES), jnp.float32)
        band_dotted = jnp.zeros((band, LANES), jnp.float32)
        for k in range(steps):
            at = slice(k * LANES, (k + 1) * LANES)
            h = hidden[at_rows, at].astype(jnp.float32)
            g = grad[at_rows, at].astype(jnp.float32)
            band_squares += h * h
            band_dotted += gain_ref[:, at] * g * h
        squares.append(band_squares)
        dotted.append(band_dotted)
    squares = jnp.concatenate(squares, axis=0)
    dotted = jnp.concatenate(dotted, axis=0)
    local_factor = jnp.sum(dotted, axis=1, keepdims=True) / (
        jnp.sum(squares, axis=1, keepdims=True) + width * EPSILON
    )
    stats[0, 0:1, :] = jnp.sum(squares.T, axis=0, keepdims=True)
    stats[0, 1:2, :] = jnp.sum(dotted.T, axis=0, keepdims=True)

    pl.semaphore_wait(barrier, tp - 1 + z)
    for mask in sorted(range(1, tp), key=lambda mask: (-bin(mask).count("1"), mask)):
        remote(
            stats.at[0], stats.at[mask], 0, stat_recv, "tp", flipped(me, mask)
        ).start()
    for step in range(1, dp):

        @pl.when(z >= step)
        def _():
            pl.semaphore_signal(
                ready, inc=1, device_id={"dp": z - step}, device_id_type=MESH
            )

    for k in range(steps):
        at = slice(k * LANES, (k + 1) * LANES)
        h = hidden[:, at].astype(jnp.float32)
        g = grad[:, at].astype(jnp.float32)
        both[0:rows, at] = (gain_ref[:, at] * g - h * local_factor).astype(jnp.bfloat16)

    def products(slot, which, target):
        out = lax.dot_general(
            both[...],
            weight[slot, pl.ds(pl.multiple_of(which * block, block), block)],
            (((1,), (1,)), ((), ())),
            preferred_element_type=jnp.float32,
        )
        target[0] = out[0:rows] + local_factor * out[rows:]
        target[1] = out[rows:]

    pair_copies = []

    def pair_step(slot):
        weight_loads[slot].wait()
        products(slot, 1 - core, pair_out.at[slot])
        products(slot, core, pair_own.at[slot])
        copy = remote(
            pair_out.at[slot], pair_in.at[slot], 1, pair_recv.at[slot], "tp", flipped(me, 1)
        )
        copy.start()
        pair_copies.append(copy)

    for slot in range(last):
        pair_step(slot)

    def relay(piece, source, target, kind, recv_sem):
        copy = remote(
            source, target, kind, recv_sem, "tp", flipped(me, order[1 + piece % 2])
        )
        copy.start()
        return copy

    early_copies = []
    pair_copies[0].wait_recv()
    if relayed:
        for piece in range(pieces):
            at = slice(piece * LANES, (piece + 1) * LANES)
            for plane in range(2):
                early_out[piece, plane] = (
                    pair_own[0, plane, 0:early, at] + pair_in[0, plane, 0:early, at]
                )
            early_copies.append(
                relay(piece, early_out.at[piece], early_in.at[piece], 2, early_recv.at[piece])
            )

    wait_bytes(stats.at[pl.ds(1, tp - 1)], stat_recv)
    total = stats[0]
    for mask in range(1, tp):
        total = total + stats[mask]
    inverse_row = lax.rsqrt(total[0:1, :] / features + EPSILON)
    factor_row = inverse_row * inverse_row * total[1:2, :] / features
    inverse = jnp.broadcast_to(inverse_row, (LANES, rows)).T
    factor = jnp.broadcast_to(factor_row, (LANES, rows)).T

    def chip_piece(slot, piece, low=0, high=rows):
        at = slice(piece * LANES, (piece + 1) * LANES)
        own, got = pair_own.at[slot, :, low:high, at], pair_in.at[slot, :, low:high, at]
        gained = own[0] + got[0]
        plain = own[1] + got[1]
        chip_out[slot, piece, low:high] = inverse[low:high] * (
            gained - factor[low:high] * plain
        )

    def send(slot, piece, part):
        at = pl.ds(*parts[part])
        remote(
            chip_out.at[slot, piece, at],
            chip_in.at[slot, piece, at],
            3,
            chip_recv,
            "tp",
            flipped(me, order[slot]),
        ).start()

    relay_copies = []
    if relayed:
        for part in range(1, len(parts)):
            low, size = parts[part]
            for piece in range(pieces):
                chip_piece(0, piece, low, low + size)
                relay_copies.append(
                    relay(
                        piece,
                        chip_out.at[0, piece, pl.ds(low, size)],
                        relay_in.at[piece, pl.ds(low, size)],
                        4,
                        relay_recv.at[piece, part - 1],
                    )
                )
    else:
        for piece in range(pieces):
            chip_piece(0, piece)
            send(0, piece, 0)
    for slot in range(1, last):
        pair_copies[slot].wait_recv()
        for piece in range(pieces):
            chip_piece(slot, piece)
            if not relayed or piece % 2 == slot - 1:
                for part in range(len(parts)):
                    send(slot, piece, part)

    for k in range(steps):
        at = slice(k * LANES, (k + 1) * LANES)
        h = hidden[:, at].astype(jnp.float32)
        g = grad[:, at].astype(jnp.float32)
        sums[0, :, at] = jnp.sum(g * h * inverse, axis=0, keepdims=True)
    sum_copies = []
    for step in range(dp - 1, 0, -1):
        copy = remote(
            sums.at[0], sums.at[step], 5, sum_recv, "dp", lax.rem(z + step, dp)
        )
        pl.when(z + step >= dp)(copy.start)
        sum_copies.append((step, copy))

    pair_step(last)

    for k in range(steps):
        at = slice(k * LANES, (k + 1) * LANES)
        h = hidden[:, at].astype(jnp.float32)
        g = grad[:, at].astype(jnp.float32)
        value = inverse * (gain_ref[:, at] * g - h * factor)
        resid[:, at] = value.astype(jnp.bfloat16)

    @pl.when(z < dp - 1)
    def _():
        pl.semaphore_wait(ready, dp - 1 - z)

    for step, copy in sum_copies:
        pl.when(z + step < dp)(copy.start)

    if relayed:
        for piece in range(pieces):
            slot = 2 - piece % 2
            early_copies[piece].wait_recv()
            chip_out[slot, piece, 0:early] = chip_out[slot, piece, 0:early] + inverse[
                0:early
            ] * (early_in[piece, 0] - factor[0:early] * early_in[piece, 1])
            send(slot, piece, 0)
        for i, copy in enumerate(relay_copies):
            part, piece = 1 + i // pieces, i % pieces
            slot = 2 - piece % 2
            low, size = parts[part]
            at = slice(low, low + size)
            copy.wait_recv()
            chip_out[slot, piece, at] = chip_out[slot, piece, at] + relay_in[piece, at]
            send(slot, piece, part)

    pair_copies[last].wait_recv()
    for piece in range(pieces):
        chip_piece(last, piece)

    wait_bytes(sums.at[pl.ds(1, dp - 1)], sum_recv)
    gain_total = sums[0]
    for step in range(1, dp):
        gain_total = gain_total + sums[step]
    gain_out[...] = gain_total

    first = 1 if relayed else 0
    wait_bytes(chip_in.at[pl.ds(first, last - first)], chip_recv)
    for piece in range(pieces):
        result = chip_out[last, piece]
        for slot in range(first, last):
            result = result + chip_in[slot, piece]
        attn[:, piece * LANES : (piece + 1) * LANES] = result.astype(jnp.bfloat16)

    wait_bytes(stats.at[pl.ds(1, tp - 1)], send_sem.at[0])
    wait_bytes(pair_out, send_sem.at[1])
    wait_bytes(chip_in.at[pl.ds(first, last - first)], send_sem.at[3])
    if relayed:
        wait_bytes(early_out, send_sem.at[2])
        wait_bytes(relay_in.at[:, pl.ds(early, rows - early)], send_sem.at[4])
    wait_bytes(sums.at[pl.ds(1, dp - 1)], send_sem.at[5])


def write_results(resid, attn, gain, resid_out, attn_out, gain_out, sem):
    copies = [
        pltpu.make_async_copy(source, target, sem.at[i])
        for i, (source, target) in enumerate(
            ((resid, resid_out), (attn, attn_out), (gain, gain_out))
        )
    ]
    for copy in copies:
        copy.start()
    for copy in copies:
        copy.wait()


def on_device(tp, dp, features, grad_out, hidden_sum, norm_gain, out_weight):
    rows, width = grad_out.shape
    block = out_weight.shape[0] // tp
    half = tp // 2
    pieces = block // LANES
    parts = cuts(rows, half == 4 and pieces % 2 == 0)
    early = parts[0][1]
    anywhere = pl.BlockSpec(memory_space=pltpu.HBM)
    vmem = pl.BlockSpec(memory_space=pltpu.VMEM)
    dma = pltpu.SemaphoreType.DMA
    resid, attn, gain = pl.pallas_call(
        functools.partial(kernel, tp, dp, features),
        out_shape=(
            jax.ShapeDtypeStruct((rows, width), jnp.bfloat16),
            jax.ShapeDtypeStruct((rows, block), jnp.bfloat16),
            jax.ShapeDtypeStruct((1, width), jnp.float32),
        ),
        in_specs=[anywhere, anywhere, anywhere, anywhere],
        out_specs=(vmem, vmem, vmem),
        scratch_shapes=[
            pltpu.VMEM((rows, width), jnp.bfloat16),
            pltpu.VMEM((2 * rows, width), jnp.bfloat16),
            pltpu.VMEM((1, width), jnp.float32),
            pltpu.VMEM((half, 2 * block, width), jnp.bfloat16),
            pltpu.VMEM((tp, 2, rows), jnp.float32),
            pltpu.VMEM((half, 2, rows, block), jnp.float32),
            pltpu.VMEM((half, 2, rows, block), jnp.float32),
            pltpu.VMEM((half, 2, rows, block), jnp.float32),
            pltpu.VMEM((half, pieces, rows, LANES), jnp.float32),
            pltpu.VMEM((half, pieces, rows, LANES), jnp.float32),
            pltpu.VMEM((pieces, 2, early, LANES), jnp.float32),
            pltpu.VMEM((pieces, 2, early, LANES), jnp.float32),
            pltpu.VMEM((pieces, rows, LANES), jnp.float32),
            pltpu.VMEM((dp, 1, width), jnp.float32),
            dma((BANDS + 1,)),
            dma((half,)),
            dma((6,)),
            pltpu.SemaphoreType.DMA,
            dma((half,)),
            dma((pieces,)),
            dma((pieces, max(len(parts) - 1, 1))),
            pltpu.SemaphoreType.DMA,
            pltpu.SemaphoreType.DMA,
            pltpu.SemaphoreType.REGULAR,
        ],
        compiler_params=pltpu.CompilerParams(
            collective_id=0, has_side_effects=True, vmem_limit_bytes=52 * 2**20
        ),
        name="backward",
    )(
        pltpu.with_memory_space_constraint(grad_out, pltpu.HBM),
        pltpu.with_memory_space_constraint(hidden_sum, pltpu.HBM),
        pltpu.with_memory_space_constraint(norm_gain.reshape(1, width), pltpu.HBM),
        pltpu.with_memory_space_constraint(out_weight, pltpu.HBM),
    )
    resid, attn, gain = pl.pallas_call(
        write_results,
        out_shape=(
            jax.ShapeDtypeStruct((rows, width), jnp.bfloat16),
            jax.ShapeDtypeStruct((rows, block), jnp.bfloat16),
            jax.ShapeDtypeStruct((1, width), jnp.float32),
        ),
        in_specs=[vmem, vmem, vmem],
        out_specs=(anywhere, anywhere, anywhere),
        scratch_shapes=[dma((3,))],
        compiler_params=pltpu.CompilerParams(vmem_limit_bytes=4 * 2**20),
        name="write_results",
    )(resid, attn, gain)
    return resid, attn, gain.reshape(width)


def solution(mesh):
    tp, dp = mesh.shape["tp"], mesh.shape["dp"]

    def whole(grad_out, hidden_sum, norm_gain, out_weight):
        features = grad_out.shape[1]
        return jax.shard_map(
            functools.partial(on_device, tp, dp, features),
            mesh=mesh,
            in_specs=(P("dp", "tp"), P("dp", "tp"), P("tp"), P(None, "tp")),
            out_specs=(P("dp", "tp"), P("dp", "tp"), P("tp")),
            check_vma=False,
        )(grad_out, hidden_sum, norm_gain, out_weight)

    return whole
```

time: 16.5 us -> 16.1 us (0.976)
  Pallas kernels: 15.8 us -> 15.3 us
    pallas_call x1, Pallas kernels: 14.9 us -> 14.5 us  [on_device(): pl.pallas_call(functools.partial(kernel, tp, dp, features), out_shape=(ja...]
where the time goes in v2:
time: 16.1 us; the launch traced here: 15.9 us
  Pallas kernels  15.3 us (95%)
  between operations  0.64 us (4%)
    pallas_call x1, Pallas kernels, on_device(): pl.pallas_call(functools.partial(kernel, tp, dp, features), out_shape=(ja...  14.5 us
    pallas_call x1, Pallas kernels, on_device(): pl.pallas_call(write_results, out_shape=(jax.ShapeDtypeStruct((rows, widt...  0.83 us

profile of v2, /device:TPU:0, one launch (start us, length us, event | category | flops | bytes accessed | tf_op | source)
XLA Modules:
  0.0 15.9 jit_solution(15310150478795684012)
XLA Ops:
  0.6 14.5 %backward.1 = (bf16[128,2048]{1,0:T(8,128)(2,1)S(1)}, bf16[128,256]{1,0:T(8,128)(2,1)S(1)}, f32[1,2048]{1,0:T(1,128)S(1)}) custom-call(bf16[128,2048]{1,0:T(8,128)(2,1)} %grad_hbm.1, bf16[128,2048]{1,0:T(8,128)(2,1)} %hidden_hbm.1, f32[1,2048]{1,0:T(1,128)} %bitcast.2, bf16[2048,2048]{1,0:T(8,128)(2,1)} %weight_hbm.1), custom_call_target="tpu_custom_call" | custom-call | tf_op jit(solution)/shard_map/backward/pallas_call | solution.py:342
  15.1 0.8 %write_results.1 = (bf16[128,2048]{1,0:T(8,128)(2,1)}, bf16[128,256]{1,0:T(8,128)(2,1)}, f32[1,2048]{1,0:T(1,128)}) custom-call(bf16[128,2048]{1,0:T(8,128)(2,1)S(1)} %get-tuple-element.9.resid, bf16[128,256]{1,0:T(8,128)(2,1)S(1)} %get-tuple-element.10.attn, f32[1,2048]{1,0:T(1,128)S(1)} %get-tuple-element.11.gain), custom_call_target="tpu_custom_call" | custom-call | tf_op jit(solution)/shard_map/write_results/pallas_call | solution.py:387

commit v3 on v2

--- a/solution.py
+++ b/solution.py
@@ -34,7 +34,7 @@
     grad_hbm, hidden_hbm, gain_hbm, weight_hbm,
     resid, attn, gain_out,
     grad, both, gain_ref, weight, stats, pair_out, pair_in, pair_own, chip_out, chip_in,
-    early_out, early_in, relay_in, sums,
+    early_out, early_in, relay_in, sums, crossed,
     load_sem, weight_sem, send_sem, stat_recv, pair_recv, early_recv, relay_recv, chip_recv,
     sum_recv, ready,
 ):
@@ -156,15 +156,18 @@
 
     def pair_step(slot):
         weight_loads[slot].wait()
-        products(slot, 1 - core, pair_out.at[slot])
-        products(slot, core, pair_own.at[slot])
         copy = remote(
             pair_out.at[slot], pair_in.at[slot], 1, pair_recv.at[slot], "tp", flipped(me, 1)
         )
-        copy.start()
+        products(slot, 1 - core, pair_out.at[slot])
+        if slot < 0:
+            copy.start()
+        products(slot, core, pair_own.at[slot])
+        if slot >= 0:
+            copy.start()
         pair_copies.append(copy)
 
-    for slot in range(last):
+    for slot in range(min(last, 2)):
         pair_step(slot)
 
     def relay(piece, source, target, kind, recv_sem):
@@ -187,6 +190,13 @@
                 relay(piece, early_out.at[piece], early_in.at[piece], 2, early_recv.at[piece])
             )
 
+    for slot in range(2, last):
+        pair_step(slot)
+
+    for k in range(steps):
+        at = slice(k * LANES, (k + 1) * LANES)
+        crossed[:, at] = hidden[:, at].astype(jnp.float32) * grad[:, at].astype(jnp.float32)
+
     wait_bytes(stats.at[pl.ds(1, tp - 1)], stat_recv)
     total = stats[0]
     for mask in range(1, tp):
@@ -195,6 +205,17 @@
     factor_row = inverse_row * inverse_row * total[1:2, :] / features
     inverse = jnp.broadcast_to(inverse_row, (LANES, rows)).T
     factor = jnp.broadcast_to(factor_row, (LANES, rows)).T
+
+    for k in range(steps):
+        at = slice(k * LANES, (k + 1) * LANES)
+        sums[0, :, at] = jnp.sum(crossed[:, at] * inverse, axis=0, keepdims=True)
+    sum_copies = []
+    for step in range(1, dp):
+        copy = remote(
+            sums.at[0], sums.at[step], 5, sum_recv, "dp", lax.rem(z + step, dp)
+        )
+        pl.when(z + step >= dp)(copy.start)
+        sum_copies.append((step, copy))
 
     def chip_piece(slot, piece, low=0, high=rows):
         at = slice(piece * LANES, (piece + 1) * LANES)
@@ -243,19 +264,6 @@
                 for part in range(len(parts)):
                     send(slot, piece, part)
 
-    for k in range(steps):
-        at = slice(k * LANES, (k + 1) * LANES)
-        h = hidden[:, at].astype(jnp.float32)
-        g = grad[:, at].astype(jnp.float32)
-        sums[0, :, at] = jnp.sum(g * h * inverse, axis=0, keepdims=True)
-    sum_copies = []
-    for step in range(dp - 1, 0, -1):
-        copy = remote(
-            sums.at[0], sums.at[step], 5, sum_recv, "dp", lax.rem(z + step, dp)
-        )
-        pl.when(z + step >= dp)(copy.start)
-        sum_copies.append((step, copy))
-
     pair_step(last)
 
     for k in range(steps):
@@ -269,7 +277,7 @@
     def _():
         pl.semaphore_wait(ready, dp - 1 - z)
 
-    for step, copy in sum_copies:
+    for step, copy in reversed(sum_copies):
         pl.when(z + step < dp)(copy.start)
 
     if relayed:
@@ -363,6 +371,7 @@
             pltpu.VMEM((pieces, 2, early, LANES), jnp.float32),
             pltpu.VMEM((pieces, rows, LANES), jnp.float32),
             pltpu.VMEM((dp, 1, width), jnp.float32),
+            pltpu.VMEM((rows, width), jnp.float32),
             dma((BANDS + 1,)),
             dma((half,)),
             dma((6,)),

time: 16.1 us -> 15.5 us (0.963)
  Pallas kernels: 15.3 us -> 14.7 us
    pallas_call x1, Pallas kernels: 14.5 us -> 13.8 us  [on_device(): pl.pallas_call(functools.partial(kernel, tp, dp, features), out_shape=(ja...]
where the time goes in v3:
time: 15.5 us; the launch traced here: 15.3 us
  Pallas kernels  14.7 us (95%)
  between operations  0.64 us (4%)
    pallas_call x1, Pallas kernels, on_device(): pl.pallas_call(functools.partial(kernel, tp, dp, features), out_shape=(ja...  13.8 us
    pallas_call x1, Pallas kernels, on_device(): pl.pallas_call(write_results, out_shape=(jax.ShapeDtypeStruct((rows, widt...  0.83 us

profile of v3, /device:TPU:0, one launch (start us, length us, event | category | flops | bytes accessed | tf_op | source)
XLA Modules:
  0.0 15.3 jit_solution(421866210474837055)
XLA Ops:
  0.6 13.8 %backward.1 = (bf16[128,2048]{1,0:T(8,128)(2,1)S(1)}, bf16[128,256]{1,0:T(8,128)(2,1)S(1)}, f32[1,2048]{1,0:T(1,128)S(1)}) custom-call(bf16[128,2048]{1,0:T(8,128)(2,1)} %grad_hbm.1, bf16[128,2048]{1,0:T(8,128)(2,1)} %hidden_hbm.1, f32[1,2048]{1,0:T(1,128)} %bitcast.2, bf16[2048,2048]{1,0:T(8,128)(2,1)} %weight_hbm.1), custom_call_target="tpu_custom_call" | custom-call | tf_op jit(solution)/shard_map/backward/pallas_call | solution.py:350
  14.5 0.8 %write_results.1 = (bf16[128,2048]{1,0:T(8,128)(2,1)}, bf16[128,256]{1,0:T(8,128)(2,1)}, f32[1,2048]{1,0:T(1,128)}) custom-call(bf16[128,2048]{1,0:T(8,128)(2,1)S(1)} %get-tuple-element.9.resid, bf16[128,256]{1,0:T(8,128)(2,1)S(1)} %get-tuple-element.10.attn, f32[1,2048]{1,0:T(1,128)S(1)} %get-tuple-element.11.gain), custom_call_target="tpu_custom_call" | custom-call | tf_op jit(solution)/shard_map/write_results/pallas_call | solution.py:396

commit v4 on v3

--- a/solution.py
+++ b/solution.py
@@ -11,6 +11,9 @@
 MESH = pl.DeviceIdType.MESH
 LANES = 128
 BANDS = 4
+PARTS = 4
+EARLY = 2
+HALVES = 4
 
 
 def flipped(index, mask):
@@ -22,11 +25,9 @@
     return result
 
 
-def cuts(rows, relayed):
-    if not relayed:
-        return [(0, rows)]
-    half, quarter = rows // 2, rows // 4
-    return [(0, half), (half, quarter), (half + quarter, quarter)]
+def cuts(rows, number):
+    part = rows // number
+    return [(i * part, part) for i in range(number)]
 
 
 def kernel(
@@ -34,8 +35,8 @@
     grad_hbm, hidden_hbm, gain_hbm, weight_hbm,
     resid, attn, gain_out,
     grad, both, gain_ref, weight, stats, pair_out, pair_in, pair_own, chip_out, chip_in,
-    early_out, early_in, relay_in, sums, crossed,
-    load_sem, weight_sem, send_sem, stat_recv, pair_recv, early_recv, relay_recv, chip_recv,
+    early_out, early_in, second_in, relay_in, handed, sums, crossed,
+    load_sem, weight_sem, send_sem, stat_recv, pair_recv, first_recv, early_recv, relay_recv, handed_recv, chip_recv,
     sum_recv, ready,
 ):
     me = lax.axis_index("tp")
@@ -50,8 +51,7 @@
     order = sorted(range(0, tp, 2), key=lambda mask: (-bin(mask).count("1"), mask))
     last = len(order) - 1
     relayed = len(order) == 4 and pieces % 2 == 0
-    parts = cuts(rows, relayed)
-    early = parts[0][1]
+    parts, halves = cuts(rows, PARTS), cuts(rows, HALVES)
 
     def remote(source, target, kind, recv_sem, axis, index):
         return pltpu.make_async_remote_copy(
@@ -153,42 +153,102 @@
         target[1] = out[rows:]
 
     pair_copies = []
+    first_copies = [] if not relayed else [
+        remote(
+            pair_out.at[0, :, pl.ds(low, size)],
+            pair_in.at[0, :, pl.ds(low, size)],
+            1,
+            first_recv.at[part],
+            "tp",
+            flipped(me, 1),
+        )
+        for part, (low, size) in enumerate(halves)
+    ]
 
     def pair_step(slot):
         weight_loads[slot].wait()
-        copy = remote(
-            pair_out.at[slot], pair_in.at[slot], 1, pair_recv.at[slot], "tp", flipped(me, 1)
-        )
         products(slot, 1 - core, pair_out.at[slot])
-        if slot < 0:
+        products(slot, core, pair_own.at[slot])
+        if slot == 0 and relayed:
+            for copy in first_copies:
+                copy.start()
+            pair_copies.append(None)
+        else:
+            copy = remote(
+                pair_out.at[slot],
+                pair_in.at[slot],
+                1,
+                pair_recv.at[slot],
+                "tp",
+                flipped(me, 1),
+            )
             copy.start()
-        products(slot, core, pair_own.at[slot])
-        if slot >= 0:
-            copy.start()
-        pair_copies.append(copy)
+            pair_copies.append(copy)
 
     for slot in range(min(last, 2)):
         pair_step(slot)
 
-    def relay(piece, source, target, kind, recv_sem):
-        copy = remote(
-            source, target, kind, recv_sem, "tp", flipped(me, order[1 + piece % 2])
-        )
-        copy.start()
-        return copy
-
-    early_copies = []
-    pair_copies[0].wait_recv()
+    def early_relay(piece, part):
+        return remote(
+            early_out.at[piece, part],
+            early_in.at[piece, part],
+            2,
+            early_recv.at[piece, part],
+            "tp",
+            flipped(me, order[1 + piece % 2] + 1),
+        )
+
+    def late_relay(piece, half):
+        at = pl.ds(*halves[half])
+        return remote(
+            chip_out.at[0, piece, at],
+            relay_in.at[piece, at],
+            2,
+            relay_recv.at[piece, half],
+            "tp",
+            flipped(me, order[1 + piece % 2]),
+        )
+
+    def second_relay(piece, part):
+        at = pl.ds(*parts[part])
+        return remote(
+            chip_out.at[0, piece, at],
+            second_in.at[piece, at],
+            6,
+            early_recv.at[piece, part],
+            "tp",
+            flipped(me, order[1 + piece % 2] + 1),
+        )
+
+    early_relays = [(part, piece) for part in range(EARLY) for piece in range(pieces)]
+    second_relays = [
+        (part, piece) for part in range(EARLY, PARTS) for piece in range(pieces)
+    ]
+    late_relays = [(half, piece) for half in range(HALVES) for piece in range(pieces)]
+    if not relayed:
+        pair_copies[0].wait_recv()
     if relayed:
-        for piece in range(pieces):
-            at = slice(piece * LANES, (piece + 1) * LANES)
-            for plane in range(2):
-                early_out[piece, plane] = (
-                    pair_own[0, plane, 0:early, at] + pair_in[0, plane, 0:early, at]
-                )
-            early_copies.append(
-                relay(piece, early_out.at[piece], early_in.at[piece], 2, early_recv.at[piece])
-            )
+
+        @pl.when(core == 1)
+        def _():
+            for copy in first_copies:
+                copy.wait_recv()
+
+        @pl.when(core == 0)
+        def _():
+            for part, piece in early_relays:
+                low, size = parts[part]
+                if piece == 0 and part * HALVES % PARTS == 0:
+                    first_copies[part * HALVES // PARTS].wait_recv()
+                at = slice(piece * LANES, (piece + 1) * LANES)
+                for plane in range(2):
+                    early_out[piece, part, plane] = (
+                        pair_own[0, plane, low : low + size, at]
+                        + pair_in[0, plane, low : low + size, at]
+                    )
+                early_relay(piece, part).start()
+            for half in range((EARLY - 1) * HALVES // PARTS + 1, HALVES):
+                first_copies[half].wait_recv()
 
     for slot in range(2, last):
         pair_step(slot)
@@ -206,17 +266,6 @@
     inverse = jnp.broadcast_to(inverse_row, (LANES, rows)).T
     factor = jnp.broadcast_to(factor_row, (LANES, rows)).T
 
-    for k in range(steps):
-        at = slice(k * LANES, (k + 1) * LANES)
-        sums[0, :, at] = jnp.sum(crossed[:, at] * inverse, axis=0, keepdims=True)
-    sum_copies = []
-    for step in range(1, dp):
-        copy = remote(
-            sums.at[0], sums.at[step], 5, sum_recv, "dp", lax.rem(z + step, dp)
-        )
-        pl.when(z + step >= dp)(copy.start)
-        sum_copies.append((step, copy))
-
     def chip_piece(slot, piece, low=0, high=rows):
         at = slice(piece * LANES, (piece + 1) * LANES)
         own, got = pair_own.at[slot, :, low:high, at], pair_in.at[slot, :, low:high, at]
@@ -226,8 +275,8 @@
             gained - factor[low:high] * plain
         )
 
-    def send(slot, piece, part):
-        at = pl.ds(*parts[part])
+    def send(slot, piece, low=0, size=rows):
+        at = pl.ds(low, size)
         remote(
             chip_out.at[slot, piece, at],
             chip_in.at[slot, piece, at],
@@ -237,32 +286,52 @@
             flipped(me, order[slot]),
         ).start()
 
-    relay_copies = []
     if relayed:
-        for part in range(1, len(parts)):
-            low, size = parts[part]
-            for piece in range(pieces):
+
+        @pl.when(core == 0)
+        def _():
+            for part, piece in second_relays:
+                low, size = parts[part]
                 chip_piece(0, piece, low, low + size)
-                relay_copies.append(
-                    relay(
-                        piece,
-                        chip_out.at[0, piece, pl.ds(low, size)],
-                        relay_in.at[piece, pl.ds(low, size)],
-                        4,
-                        relay_recv.at[piece, part - 1],
-                    )
-                )
+                second_relay(piece, part).start()
+
+    if relayed:
+
+        @pl.when(core == 1)
+        def _():
+            for half, piece in late_relays:
+                low, size = halves[half]
+                chip_piece(0, piece, low, low + size)
+                late_relay(piece, half).start()
+
     else:
         for piece in range(pieces):
             chip_piece(0, piece)
-            send(0, piece, 0)
+            send(0, piece)
+    for k in range(steps):
+        at = slice(k * LANES, (k + 1) * LANES)
+        sums[0, :, at] = jnp.sum(crossed[:, at] * inverse, axis=0, keepdims=True)
+    sum_copies = []
+    for step in range(1, dp):
+        copy = remote(
+            sums.at[0], sums.at[step], 4, sum_recv, "dp", lax.rem(z + step, dp)
+        )
+        pl.when(z + step >= dp)(copy.start)
+        sum_copies.append((step, copy))
+
+    def hand(slot, piece):
+        return remote(
+            chip_out.at[slot, piece], handed.at[piece], 5, handed_recv, "tp", flipped(me, 1)
+        )
+
     for slot in range(1, last):
         pair_copies[slot].wait_recv()
         for piece in range(pieces):
             chip_piece(slot, piece)
             if not relayed or piece % 2 == slot - 1:
-                for part in range(len(parts)):
-                    send(slot, piece, part)
+                send(slot, piece)
+            else:
+                pl.when(core == 0)(hand(slot, piece).start)
 
     pair_step(last)
 
@@ -273,29 +342,44 @@
         value = inverse * (gain_ref[:, at] * g - h * factor)
         resid[:, at] = value.astype(jnp.bfloat16)
 
+    if relayed:
+
+        @pl.when(core == 1)
+        def _():
+            wait_bytes(handed, handed_recv)
+            for part, piece in early_relays + second_relays:
+                low, size = parts[part]
+                slot, at = 2 - piece % 2, slice(low, low + size)
+                if part < EARLY:
+                    early_relay(piece, part).wait_recv()
+                    got = inverse[at] * (
+                        early_in[piece, part, 0] - factor[at] * early_in[piece, part, 1]
+                    )
+                else:
+                    second_relay(piece, part).wait_recv()
+                    got = second_in[piece, at]
+                handed[piece, at] = handed[piece, at] + got
+                remote(
+                    handed.at[piece, pl.ds(low, size)],
+                    chip_in.at[slot, piece, pl.ds(low, size)],
+                    5,
+                    chip_recv,
+                    "tp",
+                    flipped(me, order[slot] + 1),
+                ).start()
+            for half, piece in late_relays:
+                low, size = halves[half]
+                slot, at = 2 - piece % 2, slice(low, low + size)
+                late_relay(piece, half).wait_recv()
+                chip_out[slot, piece, at] = chip_out[slot, piece, at] + relay_in[piece, at]
+                send(slot, piece, low, size)
+
     @pl.when(z < dp - 1)
     def _():
         pl.semaphore_wait(ready, dp - 1 - z)
 
     for step, copy in reversed(sum_copies):
         pl.when(z + step < dp)(copy.start)
-
-    if relayed:
-        for piece in range(pieces):
-            slot = 2 - piece % 2
-            early_copies[piece].wait_recv()
-            chip_out[slot, piece, 0:early] = chip_out[slot, piece, 0:early] + inverse[
-                0:early
-            ] * (early_in[piece, 0] - factor[0:early] * early_in[piece, 1])
-            send(slot, piece, 0)
-        for i, copy in enumerate(relay_copies):
-            part, piece = 1 + i // pieces, i % pieces
-            slot = 2 - piece % 2
-            low, size = parts[part]
-            at = slice(low, low + size)
-            copy.wait_recv()
-            chip_out[slot, piece, at] = chip_out[slot, piece, at] + relay_in[piece, at]
-            send(slot, piece, part)
 
     pair_copies[last].wait_recv()
     for piece in range(pieces):
@@ -317,11 +401,23 @@
 
     wait_bytes(stats.at[pl.ds(1, tp - 1)], send_sem.at[0])
     wait_bytes(pair_out, send_sem.at[1])
-    wait_bytes(chip_in.at[pl.ds(first, last - first)], send_sem.at[3])
+    wait_bytes(sums.at[pl.ds(1, dp - 1)], send_sem.at[4])
     if relayed:
-        wait_bytes(early_out, send_sem.at[2])
-        wait_bytes(relay_in.at[:, pl.ds(early, rows - early)], send_sem.at[4])
-    wait_bytes(sums.at[pl.ds(1, dp - 1)], send_sem.at[5])
+        wait_bytes(handed, send_sem.at[5])
+
+        @pl.when(core == 0)
+        def _():
+            wait_bytes(chip_in.at[1], send_sem.at[3])
+            wait_bytes(early_out, send_sem.at[2])
+            wait_bytes(second_in.at[:, pl.ds(parts[EARLY][0], rows - parts[EARLY][0])], send_sem.at[6])
+
+        @pl.when(core == 1)
+        def _():
+            wait_bytes(chip_in.at[pl.ds(1, 2)], send_sem.at[3])
+            wait_bytes(relay_in, send_sem.at[2])
+
+    else:
+        wait_bytes(chip_in.at[pl.ds(0, last)], send_sem.at[3])
 
 
 def write_results(resid, attn, gain, resid_out, attn_out, gain_out, sem):
@@ -342,8 +438,6 @@
     block = out_weight.shape[0] // tp
     half = tp // 2
     pieces = block // LANES
-    parts = cuts(rows, half == 4 and pieces % 2 == 0)
-    early = parts[0][1]
     anywhere = pl.BlockSpec(memory_space=pltpu.HBM)
     vmem = pl.BlockSpec(memory_space=pltpu.VMEM)
     dma = pltpu.SemaphoreType.DMA
@@ -367,18 +461,22 @@
             pltpu.VMEM((half, 2, rows, block), jnp.float32),
             pltpu.VMEM((half, pieces, rows, LANES), jnp.float32),
             pltpu.VMEM((half, pieces, rows, LANES), jnp.float32),
-            pltpu.VMEM((pieces, 2, early, LANES), jnp.float32),
-            pltpu.VMEM((pieces, 2, early, LANES), jnp.float32),
+            pltpu.VMEM((pieces, EARLY, 2, rows // PARTS, LANES), jnp.float32),
+            pltpu.VMEM((pieces, EARLY, 2, rows // PARTS, LANES), jnp.float32),
+            pltpu.VMEM((pieces, rows, LANES), jnp.float32),
+            pltpu.VMEM((pieces, rows, LANES), jnp.float32),
             pltpu.VMEM((pieces, rows, LANES), jnp.float32),
             pltpu.VMEM((dp, 1, width), jnp.float32),
             pltpu.VMEM((rows, width), jnp.float32),
             dma((BANDS + 1,)),
             dma((half,)),
-            dma((6,)),
+            dma((7,)),
             pltpu.SemaphoreType.DMA,
             dma((half,)),
-            dma((pieces,)),
-            dma((pieces, max(len(parts) - 1, 1))),
+            dma((HALVES,)),
+            dma((pieces, PARTS)),
+            dma((pieces, HALVES)),
+            pltpu.SemaphoreType.DMA,
             pltpu.SemaphoreType.DMA,
             pltpu.SemaphoreType.DMA,
             pltpu.SemaphoreType.REGULAR,

time: 15.5 us -> 14.7 us (0.948)
  Pallas kernels: 14.7 us -> 13.9 us
    pallas_call x1, Pallas kernels: 13.8 us -> 13.1 us  [on_device(): pl.pallas_call(functools.partial(kernel, tp, dp, features), out_shape=(ja...]
where the time goes in v4:
time: 14.7 us; the launch traced here: 14.5 us
  Pallas kernels  13.9 us (95%)
  between operations  0.64 us (4%)
    pallas_call x1, Pallas kernels, on_device(): pl.pallas_call(functools.partial(kernel, tp, dp, features), out_shape=(ja...  13.1 us
    pallas_call x1, Pallas kernels, on_device(): pl.pallas_call(write_results, out_shape=(jax.ShapeDtypeStruct((rows, widt...  0.83 us

profile of v4, /device:TPU:0, one launch (start us, length us, event | category | flops | bytes accessed | tf_op | source)
XLA Modules:
  0.0 14.5 jit_solution(11565593345847236067)
XLA Ops:
  0.6 13.1 %backward.1 = (bf16[128,2048]{1,0:T(8,128)(2,1)S(1)}, bf16[128,256]{1,0:T(8,128)(2,1)S(1)}, f32[1,2048]{1,0:T(1,128)S(1)}) custom-call(bf16[128,2048]{1,0:T(8,128)(2,1)} %grad_hbm.1, bf16[128,2048]{1,0:T(8,128)(2,1)} %hidden_hbm.1, f32[1,2048]{1,0:T(1,128)} %bitcast.2, bf16[2048,2048]{1,0:T(8,128)(2,1)} %weight_hbm.1), custom_call_target="tpu_custom_call" | custom-call | tf_op jit(solution)/shard_map/backward/pallas_call | solution.py:444
  13.7 0.8 %write_results.1 = (bf16[128,2048]{1,0:T(8,128)(2,1)}, bf16[128,256]{1,0:T(8,128)(2,1)}, f32[1,2048]{1,0:T(1,128)}) custom-call(bf16[128,2048]{1,0:T(8,128)(2,1)S(1)} %get-tuple-element.9.resid, bf16[128,256]{1,0:T(8,128)(2,1)S(1)} %get-tuple-element.10.attn, f32[1,2048]{1,0:T(1,128)S(1)} %get-tuple-element.11.gain), custom_call_target="tpu_custom_call" | custom-call | tf_op jit(solution)/shard_map/write_results/pallas_call | solution.py:494
